TPU v7x, 32 devices: a whole 2x2x4 slice. The times are simulated.
32 devices in a mesh: clips: 1, frame: 32 (over z, y, x, core).
Axes of the slice: x: 2, y: 2, z: 4, core: 2. Of those that a mesh axis runs over, the one named last changes fastest.
Arguments:
- frame_sequence_elements: bfloat16 [32, 256, 1280], P(('clips', 'frame')), may hold values from -8 to 8
- entry_rescaling_factors: float32 [1280], replicated, may hold values from 0.5 to 1.5
- asking_projection_tensor: bfloat16 [1280, 640], replicated, may hold values from -1 to 1
- lookup_projection_tensor: bfloat16 [1280, 640], replicated, may hold values from -1 to 1
- content_projection_tensor: bfloat16 [1280, 640], replicated, may hold values from -0.15625 to 0.15625
- logit_sharpness: float32 [5], replicated, may hold values from 0.3 to 24
- final_projection_tensor: bfloat16 [640, 1280], replicated, may hold values from -0.25 to 0.25
Outputs:
- mixed: bfloat16 [32, 256, 1280], P(('clips', 'frame'))
All inputs are finite; a program needn't handle non-finite values.
Results may differ from a plain program's by a relative error of at most 0.006.
Values may be sent and summed in bfloat16 or wider, within the bound.
A program may use at most 64 MiB of HBM per device.

v0:
```python
import functools
import math

import jax
import jax.numpy as jnp
from jax import lax
from jax.experimental import pallas as pl
from jax.experimental.pallas import tpu as pltpu
from jax.sharding import PartitionSpec as P

HEADS_WIN = 5
CHANNELS_PER_ATT = 128
WINDOW = 32


epsilon = 1e-06


def quadratic_average_rescaling(values):
    return values * lax.rsqrt(jnp.mean(values * values, axis=-1, keepdims=True) + epsilon)


def project_through(
    incoming_token_vectors,
    asking_projection_tensor,
    lookup_projection_tensor,
    content_projection_tensor,
    logit_sharpness,
):
    lead = incoming_token_vectors.shape[:-1]
    flat_rows = incoming_token_vectors.reshape(-1, incoming_token_vectors.shape[-1])
    shape_heads = lead + (HEADS_WIN, CHANNELS_PER_ATT)
    asking_vectors_full = jnp.dot(
        flat_rows, asking_projection_tensor, preferred_element_type=jnp.float32
    ).reshape(shape_heads)
    k_full = jnp.dot(
        flat_rows, lookup_projection_tensor, preferred_element_type=jnp.float32
    ).reshape(shape_heads)
    v_full = jnp.dot(
        flat_rows, content_projection_tensor, preferred_element_type=jnp.float32
    ).reshape(shape_heads)
    asking_token_vectors = (
        quadratic_average_rescaling(asking_vectors_full)
        * logit_sharpness[:, None]
        / math.sqrt(CHANNELS_PER_ATT)
    ).astype(jnp.bfloat16)
    key_matrix_rows = quadratic_average_rescaling(k_full).astype(jnp.bfloat16)
    return (asking_token_vectors, key_matrix_rows, v_full.astype(jnp.bfloat16))


def softmax_bf16(scores, window_mask):
    scores = jnp.where(window_mask, scores, -1e30)
    top = jnp.max(scores, axis=-1, keepdims=True)
    expo = jnp.exp(scores - top)
    return (expo / jnp.sum(expo, axis=-1, keepdims=True)).astype(jnp.bfloat16)


def band_attention(asking_token_vectors, key_matrix_rows, value_matrix_rows):
    all_frames, positions, heads, width = asking_token_vectors.shape
    blocks = all_frames // WINDOW
    block_shape = (blocks, WINDOW, positions, heads, width)
    q_blocks = asking_token_vectors.reshape(block_shape)
    k_blocks = key_matrix_rows.reshape(block_shape)
    v_blocks = value_matrix_rows.reshape(block_shape)
    k_earlier = jnp.concatenate([jnp.zeros_like(k_blocks[:1]), k_blocks[:-1]], axis=0)
    v_earlier = jnp.concatenate([jnp.zeros_like(v_blocks[:1]), v_blocks[:-1]], axis=0)
    k_pair = jnp.concatenate([k_earlier, k_blocks], axis=1)
    v_pair = jnp.concatenate([v_earlier, v_blocks], axis=1)
    scores = jnp.einsum("bqphd,bkphd->bphqk", q_blocks, k_pair, preferred_element_type=jnp.float32)
    block_ids = jnp.arange(blocks, dtype=jnp.int32)[:, None, None]
    row_ids = jnp.arange(WINDOW, dtype=jnp.int32)[None, :, None]
    col_ids = jnp.arange(2 * WINDOW, dtype=jnp.int32)[None, None, :]
    offset = row_ids - col_ids + WINDOW
    inside = (offset >= 0) & (offset < WINDOW) & (block_ids * WINDOW - WINDOW + col_ids >= 0)
    weights = softmax_bf16(scores, inside[:, None, None])
    attended = jnp.einsum("bphqk,bkphd->bqphd", weights, v_pair, preferred_element_type=jnp.float32)
    return attended.astype(jnp.bfloat16).reshape(all_frames, positions, heads, width)


def local(
    frame_sequence_elements,
    entry_rescaling_factors,
    asking_projection_tensor,
    lookup_projection_tensor,
    content_projection_tensor,
    logit_sharpness,
    final_projection_tensor,
):
    frames_dev, seq_len, width = frame_sequence_elements.shape
    floated = frame_sequence_elements.astype(jnp.float32)
    rescaled_token_vectors = (
        quadratic_average_rescaling(floated) * entry_rescaling_factors
    ).astype(jnp.bfloat16)
    position_rows = lax.all_to_all(
        rescaled_token_vectors, "frame", split_axis=1, concat_axis=0, tiled=True
    )
    asking_token_vectors, key_matrix_rows, value_matrix_rows = project_through(
        position_rows,
        asking_projection_tensor,
        lookup_projection_tensor,
        content_projection_tensor,
        logit_sharpness,
    )
    result = band_attention(asking_token_vectors, key_matrix_rows, value_matrix_rows)
    attended = lax.all_to_all(result, "frame", split_axis=0, concat_axis=1, tiled=True)
    flat_attended = attended.reshape(frames_dev * seq_len, -1)
    summed = jnp.dot(
        flat_attended, final_projection_tensor, preferred_element_type=jnp.float32
    ) + floated.reshape(frames_dev * seq_len, width)
    return summed.astype(jnp.bfloat16).reshape(frames_dev, seq_len, width)


MESH = pl.DeviceIdType.MESH
HIGH = HEADS_WIN * CHANNELS_PER_ATT


def visiting_order(pairs):
    return sorted(range(1, pairs), key=lambda k: (-abs(k - pairs // 2), k))


def runs(slots):
    found, first = [], 0
    for i in range(1, len(slots) + 1):
        if i == len(slots) or slots[i] != slots[i - 1] + 1:
            found.append((first, i, slots[first]))
            first = i
    return found


def fused(
    devices,
    local_frames,
    sharp_ref,
    x_hbm,
    gain_ref,
    wq_hbm,
    wk_hbm,
    wv_hbm,
    wo_hbm,
    out_ref,
    x_own,
    wq,
    wk,
    wv,
    wo,
    gathered,
    q_rows,
    k_rows,
    v_rows,
    outgoing,
    returned,
    load_sem,
    send_a,
    recv_a,
    send_b,
    recv_b,
):
    me = lax.axis_index("frame")
    block, width = x_own.shape[1], x_own.shape[2]
    positions = block // local_frames
    pairs = devices // 2
    pair, side = me // 2, lax.rem(me, 2)
    partner = me + 1 - 2 * side
    order = visiting_order(pairs)

    barrier = pltpu.get_barrier_semaphore()
    for k in range(1, devices):
        pl.semaphore_signal(
            barrier, inc=1, device_id={"frame": lax.rem(me + k, devices)}, device_id_type=MESH
        )
    loads = [
        pltpu.make_async_copy(source, target, load_sem.at[i])
        for i, (source, target) in enumerate(
            ((x_hbm, x_own), (wq_hbm, wq), (wk_hbm, wk), (wv_hbm, wv), (wo_hbm, wo))
        )
    ]
    for load in loads:
        load.start()
    loads[0].wait()
    pl.semaphore_wait(barrier, devices - 1)

    def send_tokens(target, slot_here, slot_there):
        copy = pltpu.make_async_remote_copy(
            src_ref=x_own.at[target],
            dst_ref=gathered.at[slot_there],
            send_sem=send_a.at[slot_here],
            recv_sem=recv_a.at[slot_there],
            device_id={"frame": target},
            device_id_type=MESH,
        )
        copy.start()
        return copy

    def token_arrival(slot):
        return pltpu.make_async_remote_copy(
            src_ref=x_own.at[0],
            dst_ref=gathered.at[slot],
            send_sem=send_a.at[slot],
            recv_sem=recv_a.at[slot],
            device_id={"frame": partner},
            device_id_type=MESH,
        )

    sent = [send_tokens(partner, 0, side * pairs)]
    for s in range(2):
        for k in order:
            target = lax.rem(pair + k, pairs) * 2 + s
            sent.append(send_tokens(target, s * pairs + k, side * pairs + k))
    gathered[side * pairs] = x_own[me]
    for load in loads[1:]:
        load.wait()

    def project(slots):
        parts = [gathered[slot].astype(jnp.float32) for slot in slots]
        x = jnp.concatenate(parts, axis=0)
        normed = (quadratic_average_rescaling(x) * gain_ref[...].reshape(1, width)).astype(
            jnp.bfloat16
        )
        q = jnp.dot(normed, wq[...], preferred_element_type=jnp.float32)
        k = jnp.dot(normed, wk[...], preferred_element_type=jnp.float32)
        v = jnp.dot(normed, wv[...], preferred_element_type=jnp.float32)
        for h in range(HEADS_WIN):
            c = slice(h * CHANNELS_PER_ATT, (h + 1) * CHANNELS_PER_ATT)
            qs = (
                quadratic_average_rescaling(q[:, c]) * sharp_ref[h] / math.sqrt(CHANNELS_PER_ATT)
            ).astype(jnp.bfloat16)
            ks = quadratic_average_rescaling(k[:, c]).astype(jnp.bfloat16)
            vs = v[:, c].astype(jnp.bfloat16)
            for first, last, to in runs(slots):
                a = slice(first * block, last * block)
                b = slice(to * block, (to + last - first) * block)
                q_rows[b, c] = qs[a]
                k_rows[b, c] = ks[a]
                v_rows[b, c] = vs[a]

    total = devices * block

    def ids(axis):
        shape = (total, 1) if axis == 0 else (1, total)
        r = lax.broadcasted_iota(jnp.int32, shape, axis)
        slot = r // block
        slot_side = slot // pairs
        source = pair - (slot - slot_side * pairs)
        source = jnp.where(source < 0, source + pairs, source)
        owner = source * 2 + slot_side
        inner = r - slot * block
        return owner * local_frames + inner // positions, inner % positions

    t_row, p_row = ids(0)
    t_col, p_col = ids(1)
    offset = t_row - t_col
    inside = (p_row == p_col) & (offset >= 0) & (offset < WINDOW)
    half = pairs // 2
    early, late = [0] + order[: half - 1], order[half - 1 :]
    for piece in (early, late):
        for s in range(2):
            for k in piece:
                if k:
                    token_arrival(s * pairs + k).wait_recv()
        if 0 in piece:
            token_arrival((1 - side) * pairs).wait_recv()
        project(sorted(s * pairs + k for s in range(2) for k in piece))

    for h in range(HEADS_WIN):
        c = slice(h * CHANNELS_PER_ATT, (h + 1) * CHANNELS_PER_ATT)
        scores = lax.dot_general(
            q_rows[:, c], k_rows[:, c], (((1,), (1,)), ((), ())), preferred_element_type=jnp.float32
        )
        weights = softmax_bf16(scores, inside)
        attended = jnp.dot(weights, v_rows[:, c], preferred_element_type=jnp.float32)
        outgoing[:, :, c] = attended.reshape(devices, block, CHANNELS_PER_ATT).astype(jnp.bfloat16)

    def send_back(target, slot_here, slot_there):
        copy = pltpu.make_async_remote_copy(
            src_ref=outgoing.at[slot_here],
            dst_ref=returned.at[side, pair],
            send_sem=send_b.at[slot_here],
            recv_sem=recv_b.at[slot_there],
            device_id={"frame": target},
            device_id_type=MESH,
        )
        copy.start()
        return copy

    def arrival(s, k):
        return pltpu.make_async_remote_copy(
            src_ref=outgoing.at[0],
            dst_ref=returned.at[s, lax.rem(pair + k, pairs)],
            send_sem=send_b.at[0],
            recv_sem=recv_b.at[s * pairs + k],
            device_id={"frame": partner},
            device_id_type=MESH,
        )

    for k in order:
        for s in range(2):
            target = lax.rem(pair + pairs - k, pairs) * 2 + s
            sent.append(send_back(target, s * pairs + k, side * pairs + k))
    sent.append(send_back(partner, (1 - side) * pairs, side * pairs))
    returned[side, pair] = outgoing[side * pairs]
    arrival(1 - side, 0).wait_recv()
    for s in range(2):
        for k in order:
            arrival(s, k).wait_recv()
        rows = pairs * block
        mixed = returned[s].astype(jnp.float32).reshape(rows, HIGH).astype(jnp.bfloat16)
        summed = jnp.dot(mixed, wo[...], preferred_element_type=jnp.float32)
        for k in range(pairs):
            j = 2 * k + s
            out_ref[j] = (
                summed[k * block : (k + 1) * block] + x_own[j].astype(jnp.float32)
            ).astype(jnp.bfloat16)
    for copy in sent:
        copy.wait_send()


def local_fused(devices, x, gain, wq, wk, wv, sharp, wo):
    local_frames, seq_len, width = x.shape
    positions = seq_len // devices
    block = local_frames * positions
    total = devices * block
    blocks = x.reshape(local_frames, devices, positions, width)
    blocks = blocks.transpose(1, 0, 2, 3).reshape(devices, block, width)
    vmem = pl.BlockSpec(memory_space=pltpu.VMEM)
    anywhere = pl.BlockSpec(memory_space=pl.ANY)
    dma = pltpu.SemaphoreType.DMA
    out = pl.pallas_call(
        functools.partial(fused, devices, local_frames),
        out_shape=pltpu.VMEM(blocks.shape, jnp.bfloat16),
        in_specs=[pl.BlockSpec(memory_space=pltpu.SMEM), anywhere, vmem] + [anywhere] * 4,
        out_specs=vmem,
        scratch_shapes=[
            pltpu.VMEM(blocks.shape, jnp.bfloat16),
            pltpu.VMEM(wq.shape, jnp.bfloat16),
            pltpu.VMEM(wk.shape, jnp.bfloat16),
            pltpu.VMEM(wv.shape, jnp.bfloat16),
            pltpu.VMEM(wo.shape, jnp.bfloat16),
            pltpu.VMEM(blocks.shape, jnp.bfloat16),
            pltpu.VMEM((total, HIGH), jnp.bfloat16),
            pltpu.VMEM((total, HIGH), jnp.bfloat16),
            pltpu.VMEM((total, HIGH), jnp.bfloat16),
            pltpu.VMEM((devices, block, HIGH), jnp.bfloat16),
            pltpu.VMEM((2, devices // 2, block, HIGH), jnp.bfloat16),
            dma((5,)),
            dma((devices,)),
            dma((devices,)),
            dma((devices,)),
            dma((devices,)),
        ],
        compiler_params=pltpu.CompilerParams(
            collective_id=0, has_side_effects=True, vmem_limit_bytes=60 * 2**20
        ),
    )(sharp, blocks, gain, wq, wk, wv, wo)
    out = out.reshape(devices, local_frames, positions, width).transpose(1, 0, 2, 3)
    return out.reshape(x.shape)


def solution(mesh):
    devices = mesh.shape["frame"]

    def body(x, *rest):
        positions = x.shape[1] // devices
        if devices % 4 == 0 and positions % 8 == 0:
            return local_fused(devices, x, *rest)
        return local(x, *rest)

    placed = (P(("clips", "frame"), None, None), P(), P(), P(), P(), P(), P())
    return jax.shard_map(
        body,
        mesh=mesh,
        in_specs=placed,
        out_specs=P(("clips", "frame"), None, None),
        check_vma=False,
    )
```

profile of v0, /device:TPU:0, one launch (start us, length us, event | category | flops | bytes accessed | tf_op | source)
XLA Modules:
  0.0 32.5 jit_solution(16160747394424191876)
XLA Ops:
  0.0 31.7 %shard_map.73 = bf16[32,8,1280]{2,1,0:T(8,128)(2,1)S(1)} custom-call(f32[5]{0:T(128)} %sharp_ref.1, bf16[32,8,1280]{2,1,0:T(8,128)(2,1)} %bitcast.3, f32[1280]{0:T(1024)} %gain_ref.1, bf16[1280,640]{1,0:T(8,128)(2,1)} %wq_hbm.1, bf16[1280,640]{1,0:T(8,128)(2,1)} %wk_hbm.1, bf16[1280,640]{1,0:T(8,128)(2,1)} %wv_hbm.1, bf16[640,1280]{1,0:T(8,128)(2,1)} %wo_hbm.1), custom_call_target="tpu_custom_call" | custom-call | tf_op jit(solution)/shard_map/pallas_call | solution.py:327
  31.7 0.8 %copy.9 = bf16[1,256,1280]{2,1,0:T(8,128)(2,1)} copy(bf16[1,256,1280]{2,1,0:T(8,128)(2,1)S(1)} %bitcast.2) | data formatting | bytes 1310720
where the time goes:
time: 32.7 us; the launch traced here: 32.5 us
  Pallas kernels  31.7 us (97%)
  local copies, waits for them, and re-layouts  0.84 us (3%)
    pallas_call x1, Pallas kernels, local_fused(): pl.pallas_call(functools.partial(fused, devices, local_frames), out_shape...  31.7 us
    unnamed x1, local copies, waits for them, and re-layouts  0.84 us

commit v1 on v0

--- a/solution.py
+++ b/solution.py
@@ -114,19 +114,6 @@
 HIGH = HEADS_WIN * CHANNELS_PER_ATT
 
 
-def visiting_order(pairs):
-    return sorted(range(1, pairs), key=lambda k: (-abs(k - pairs // 2), k))
-
-
-def runs(slots):
-    found, first = [], 0
-    for i in range(1, len(slots) + 1):
-        if i == len(slots) or slots[i] != slots[i - 1] + 1:
-            found.append((first, i, slots[first]))
-            first = i
-    return found
-
-
 def fused(
     devices,
     local_frames,
@@ -150,6 +137,7 @@
     outgoing,
     returned,
     load_sem,
+    ready,
     send_a,
     recv_a,
     send_b,
@@ -158,16 +146,40 @@
     me = lax.axis_index("frame")
     block, width = x_own.shape[1], x_own.shape[2]
     positions = block // local_frames
-    pairs = devices // 2
-    pair, side = me // 2, lax.rem(me, 2)
+    chips = devices // 2
+    depth = chips // 4
+    chip, side = me // 2, lax.rem(me, 2)
     partner = me + 1 - 2 * side
-    order = visiting_order(pairs)
+    z, y, x = chip // 4, lax.rem(chip // 2, 2), lax.rem(chip, 2)
+
+    def other(dz, dy, dx):
+        tz = lax.rem(z + dz, depth)
+        ty = y + dy - 2 * dy * y
+        tx = x + dx - 2 * dx * x
+        above = (tz >= z) & (ty >= y) & (tx >= x)
+        below = (tz <= z) & (ty <= y) & (tx <= x)
+        return tz * 4 + ty * 2 + tx, above, below
+
+    steps = [(dz, dy, dx) for dz in range(depth) for dy in range(2) for dx in range(2)][1:]
+    far_first = sorted(steps, key=lambda s: (s[0] == 0, s[0]))
+    near_first = sorted(steps, key=lambda s: (sum(s), s[0]))
 
     barrier = pltpu.get_barrier_semaphore()
-    for k in range(1, devices):
+
+    def signal(semaphore, target):
         pl.semaphore_signal(
-            barrier, inc=1, device_id={"frame": lax.rem(me + k, devices)}, device_id_type=MESH
+            semaphore, inc=1, device_id={"frame": target}, device_id_type=MESH
         )
+
+    signal(barrier, partner)
+    for step in near_first:
+        there, above, _ = other(*step)
+
+        @pl.when(above)
+        def _():
+            signal(barrier, there * 2)
+            signal(barrier, there * 2 + 1)
+
     loads = [
         pltpu.make_async_copy(source, target, load_sem.at[i])
         for i, (source, target) in enumerate(
@@ -176,91 +188,116 @@
     ]
     for load in loads:
         load.start()
+    pl.semaphore_wait(barrier, 2 * ((z + 1) * (y + 1) * (x + 1) - 1) + 1)
+    for step in far_first:
+        there, _, below = other(*step)
+
+        @pl.when(below)
+        def _():
+            signal(ready.at[chip], there * 2)
+            signal(ready.at[chip], there * 2 + 1)
+
     loads[0].wait()
-    pl.semaphore_wait(barrier, devices - 1)
-
-    def send_tokens(target, slot_here, slot_there):
-        copy = pltpu.make_async_remote_copy(
+
+    def send_tokens(target):
+        pltpu.make_async_remote_copy(
             src_ref=x_own.at[target],
-            dst_ref=gathered.at[slot_there],
-            send_sem=send_a.at[slot_here],
-            recv_sem=recv_a.at[slot_there],
+            dst_ref=gathered.at[me],
+            send_sem=send_a,
+            recv_sem=recv_a.at[z // 2],
             device_id={"frame": target},
             device_id_type=MESH,
-        )
-        copy.start()
-        return copy
-
-    def token_arrival(slot):
-        return pltpu.make_async_remote_copy(
-            src_ref=x_own.at[0],
-            dst_ref=gathered.at[slot],
-            send_sem=send_a.at[slot],
-            recv_sem=recv_a.at[slot],
+        ).start()
+
+    send_tokens(partner)
+    for step in far_first:
+        there, _, below = other(*step)
+
+        @pl.when(below)
+        def _():
+            send_tokens(there * 2)
+
+    for step in near_first:
+        there, above, _ = other(*step)
+
+        @pl.when(above)
+        def _():
+            pl.semaphore_wait(ready.at[there], 2)
+            send_tokens(there * 2)
+
+    for step in near_first:
+        there, above, below = other(*step)
+
+        @pl.when(jnp.logical_not(above | below))
+        def _():
+            send_tokens(there * 2)
+
+    for step in far_first:
+        there, _, _ = other(*step)
+        send_tokens(there * 2 + 1)
+    gathered[me] = x_own[me]
+    for load in loads[1:]:
+        load.wait()
+
+    half = devices // 2
+    rows = half * block
+
+    def arrived(ref, semaphore):
+        pltpu.make_async_remote_copy(
+            src_ref=ref,
+            dst_ref=ref,
+            send_sem=send_a,
+            recv_sem=semaphore,
             device_id={"frame": partner},
             device_id_type=MESH,
-        )
-
-    sent = [send_tokens(partner, 0, side * pairs)]
-    for s in range(2):
-        for k in order:
-            target = lax.rem(pair + k, pairs) * 2 + s
-            sent.append(send_tokens(target, s * pairs + k, side * pairs + k))
-    gathered[side * pairs] = x_own[me]
-    for load in loads[1:]:
-        load.wait()
-
-    def project(slots):
-        parts = [gathered[slot].astype(jnp.float32) for slot in slots]
-        x = jnp.concatenate(parts, axis=0)
-        normed = (quadratic_average_rescaling(x) * gain_ref[...].reshape(1, width)).astype(
+        ).wait_recv()
+
+    def departed(ref, semaphore):
+        pltpu.make_async_remote_copy(
+            src_ref=ref,
+            dst_ref=ref,
+            send_sem=semaphore,
+            recv_sem=recv_a.at[0],
+            device_id={"frame": partner},
+            device_id_type=MESH,
+        ).wait_send()
+
+    def project(part):
+        tokens = gathered[pl.ds(part * half, half)].astype(jnp.float32).reshape(rows, width)
+        normed = (quadratic_average_rescaling(tokens) * gain_ref[...].reshape(1, width)).astype(
             jnp.bfloat16
         )
         q = jnp.dot(normed, wq[...], preferred_element_type=jnp.float32)
         k = jnp.dot(normed, wk[...], preferred_element_type=jnp.float32)
         v = jnp.dot(normed, wv[...], preferred_element_type=jnp.float32)
+        to = pl.ds(pl.multiple_of(part * rows, rows), rows)
         for h in range(HEADS_WIN):
             c = slice(h * CHANNELS_PER_ATT, (h + 1) * CHANNELS_PER_ATT)
-            qs = (
+            q_rows[to, c] = (
                 quadratic_average_rescaling(q[:, c]) * sharp_ref[h] / math.sqrt(CHANNELS_PER_ATT)
             ).astype(jnp.bfloat16)
-            ks = quadratic_average_rescaling(k[:, c]).astype(jnp.bfloat16)
-            vs = v[:, c].astype(jnp.bfloat16)
-            for first, last, to in runs(slots):
-                a = slice(first * block, last * block)
-                b = slice(to * block, (to + last - first) * block)
-                q_rows[b, c] = qs[a]
-                k_rows[b, c] = ks[a]
-                v_rows[b, c] = vs[a]
+            k_rows[to, c] = quadratic_average_rescaling(k[:, c]).astype(jnp.bfloat16)
+            v_rows[to, c] = v[:, c].astype(jnp.bfloat16)
+
+    mine = z // 2
+    arrived(gathered.at[pl.ds(0, half - 1)], recv_a.at[mine])
+    project(mine)
+    arrived(gathered.at[pl.ds(0, half)], recv_a.at[1 - mine])
+    project(1 - mine)
 
     total = devices * block
 
     def ids(axis):
         shape = (total, 1) if axis == 0 else (1, total)
         r = lax.broadcasted_iota(jnp.int32, shape, axis)
-        slot = r // block
-        slot_side = slot // pairs
-        source = pair - (slot - slot_side * pairs)
-        source = jnp.where(source < 0, source + pairs, source)
-        owner = source * 2 + slot_side
-        inner = r - slot * block
+        owner = r // block
+        inner = r - owner * block
         return owner * local_frames + inner // positions, inner % positions
 
     t_row, p_row = ids(0)
     t_col, p_col = ids(1)
     offset = t_row - t_col
     inside = (p_row == p_col) & (offset >= 0) & (offset < WINDOW)
-    half = pairs // 2
-    early, late = [0] + order[: half - 1], order[half - 1 :]
-    for piece in (early, late):
-        for s in range(2):
-            for k in piece:
-                if k:
-                    token_arrival(s * pairs + k).wait_recv()
-        if 0 in piece:
-            token_arrival((1 - side) * pairs).wait_recv()
-        project(sorted(s * pairs + k for s in range(2) for k in piece))
-
     for h in range(HEADS_WIN):
         c = slice(h * CHANNELS_PER_ATT, (h + 1) * CHANNELS_PER_ATT)
         scores = lax.dot_general(
@@ -270,48 +307,45 @@
         attended = jnp.dot(weights, v_rows[:, c], preferred_element_type=jnp.float32)
         outgoing[:, :, c] = attended.reshape(devices, block, CHANNELS_PER_ATT).astype(jnp.bfloat16)
 
-    def send_back(target, slot_here, slot_there):
-        copy = pltpu.make_async_remote_copy(
-            src_ref=outgoing.at[slot_here],
-            dst_ref=returned.at[side, pair],
-            send_sem=send_b.at[slot_here],
-            recv_sem=recv_b.at[slot_there],
+    def send_back(target):
+        pltpu.make_async_remote_copy(
+            src_ref=outgoing.at[target],
+            dst_ref=returned.at[side, chip],
+            send_sem=send_b,
+            recv_sem=recv_b.at[side],
             device_id={"frame": target},
             device_id_type=MESH,
-        )
-        copy.start()
-        return copy
-
-    def arrival(s, k):
-        return pltpu.make_async_remote_copy(
-            src_ref=outgoing.at[0],
-            dst_ref=returned.at[s, lax.rem(pair + k, pairs)],
-            send_sem=send_b.at[0],
-            recv_sem=recv_b.at[s * pairs + k],
-            device_id={"frame": partner},
-            device_id_type=MESH,
-        )
-
-    for k in order:
-        for s in range(2):
-            target = lax.rem(pair + pairs - k, pairs) * 2 + s
-            sent.append(send_back(target, s * pairs + k, side * pairs + k))
-    sent.append(send_back(partner, (1 - side) * pairs, side * pairs))
-    returned[side, pair] = outgoing[side * pairs]
-    arrival(1 - side, 0).wait_recv()
-    for s in range(2):
-        for k in order:
-            arrival(s, k).wait_recv()
-        rows = pairs * block
+        ).start()
+
+    for step in far_first:
+        there, _, _ = other(*step)
+        send_back(there * 2)
+        send_back(there * 2 + 1)
+    send_back(partner)
+    returned[side, chip] = outgoing[me]
+
+    def finish(s):
         mixed = returned[s].astype(jnp.float32).reshape(rows, HIGH).astype(jnp.bfloat16)
         summed = jnp.dot(mixed, wo[...], preferred_element_type=jnp.float32)
-        for k in range(pairs):
+        for k in range(chips):
             j = 2 * k + s
             out_ref[j] = (
                 summed[k * block : (k + 1) * block] + x_own[j].astype(jnp.float32)
             ).astype(jnp.bfloat16)
-    for copy in sent:
-        copy.wait_send()
+
+    for s in range(2):
+
+        @pl.when(side == s)
+        def _():
+            arrived(returned.at[s, pl.ds(0, chips - 1)], recv_b.at[s])
+
+        @pl.when(side != s)
+        def _():
+            arrived(returned.at[s], recv_b.at[s])
+
+        finish(s)
+    departed(x_own.at[pl.ds(0, devices - 1)], send_a)
+    departed(outgoing.at[pl.ds(0, devices - 1)], send_b)
 
 
 def local_fused(devices, x, gain, wq, wk, wv, sharp, wo):
@@ -342,10 +376,11 @@
             pltpu.VMEM((devices, block, HIGH), jnp.bfloat16),
             pltpu.VMEM((2, devices // 2, block, HIGH), jnp.bfloat16),
             dma((5,)),
-            dma((devices,)),
-            dma((devices,)),
-            dma((devices,)),
-            dma((devices,)),
+            pltpu.SemaphoreType.REGULAR((devices // 2,)),
+            dma,
+            dma((2,)),
+            dma,
+            dma((2,)),
         ],
         compiler_params=pltpu.CompilerParams(
             collective_id=0, has_side_effects=True, vmem_limit_bytes=60 * 2**20
@@ -360,7 +395,7 @@
 
     def body(x, *rest):
         positions = x.shape[1] // devices
-        if devices % 4 == 0 and positions % 8 == 0:
+        if devices % 16 == 0 and positions % 8 == 0:
             return local_fused(devices, x, *rest)
         return local(x, *rest)
 

time: 32.7 us -> 32.5 us (level)
  no operation moved by 1% of the time
where the time goes in v1:
time: 32.5 us; the launch traced here: 32.3 us
  Pallas kernels  31.5 us (97%)
  local copies, waits for them, and re-layouts  0.84 us (3%)
    pallas_call x1, Pallas kernels, local_fused(): pl.pallas_call(functools.partial(fused, devices, local_frames), out_shape...  31.5 us
    unnamed x1, local copies, waits for them, and re-layouts  0.84 us

profile of v1, /device:TPU:0, one launch (start us, length us, event | category | flops | bytes accessed | tf_op | source)
XLA Modules:
  0.0 32.3 jit_solution(18321371109705407221)
XLA Ops:
  0.0 31.5 %shard_map.73 = bf16[32,8,1280]{2,1,0:T(8,128)(2,1)S(1)} custom-call(f32[5]{0:T(128)} %sharp_ref.1, bf16[32,8,1280]{2,1,0:T(8,128)(2,1)} %bitcast.3, f32[1280]{0:T(1024)} %gain_ref.1, bf16[1280,640]{1,0:T(8,128)(2,1)} %wq_hbm.1, bf16[1280,640]{1,0:T(8,128)(2,1)} %wk_hbm.1, bf16[1280,640]{1,0:T(8,128)(2,1)} %wv_hbm.1, bf16[640,1280]{1,0:T(8,128)(2,1)} %wo_hbm.1), custom_call_target="tpu_custom_call" | custom-call | tf_op jit(solution)/shard_map/pallas_call | solution.py:361
  31.5 0.8 %copy.9 = bf16[1,256,1280]{2,1,0:T(8,128)(2,1)} copy(bf16[1,256,1280]{2,1,0:T(8,128)(2,1)S(1)} %bitcast.2) | data formatting | bytes 1310720

commit v2 on v1

--- a/solution.py
+++ b/solution.py
@@ -117,30 +117,37 @@
 def fused(
     devices,
     local_frames,
-    sharp_ref,
+    sharp_hbm,
     x_hbm,
-    gain_ref,
+    gain_hbm,
     wq_hbm,
     wk_hbm,
     wv_hbm,
     wo_hbm,
     out_ref,
+    sharp_ref,
+    gain_ref,
     x_own,
     wq,
     wk,
     wv,
     wo,
     gathered,
+    extra,
     q_rows,
     k_rows,
     v_rows,
     outgoing,
+    outgoing_extra,
     returned,
     load_sem,
     ready,
     send_a,
+    send_x,
     recv_a,
+    recv_x,
     send_b,
+    send_c,
     recv_b,
 ):
     me = lax.axis_index("frame")
@@ -148,9 +155,12 @@
     positions = block // local_frames
     chips = devices // 2
     depth = chips // 4
+    half = devices // 2
+    rows = half * block
     chip, side = me // 2, lax.rem(me, 2)
     partner = me + 1 - 2 * side
     z, y, x = chip // 4, lax.rem(chip // 2, 2), lax.rem(chip, 2)
+    low = me < half
 
     def other(dz, dy, dx):
         tz = lax.rem(z + dz, depth)
@@ -164,6 +174,8 @@
     far_first = sorted(steps, key=lambda s: (s[0] == 0, s[0]))
     near_first = sorted(steps, key=lambda s: (sum(s), s[0]))
 
+    x_load = pltpu.make_async_copy(x_hbm, x_own, load_sem.at[0])
+    x_load.start()
     barrier = pltpu.get_barrier_semaphore()
 
     def signal(semaphore, target):
@@ -181,14 +193,22 @@
             signal(barrier, there * 2 + 1)
 
     loads = [
-        pltpu.make_async_copy(source, target, load_sem.at[i])
+        pltpu.make_async_copy(source, target, load_sem.at[i + 1])
         for i, (source, target) in enumerate(
-            ((x_hbm, x_own), (wq_hbm, wq), (wk_hbm, wk), (wv_hbm, wv), (wo_hbm, wo))
+            (
+                (sharp_hbm, sharp_ref),
+                (gain_hbm, gain_ref),
+                (wq_hbm, wq),
+                (wk_hbm, wk),
+                (wv_hbm, wv),
+                (wo_hbm, wo),
+            )
         )
     ]
     for load in loads:
         load.start()
-    pl.semaphore_wait(barrier, 2 * ((z + 1) * (y + 1) * (x + 1) - 1) + 1)
+    with jax.named_scope("barrier"):
+        pl.semaphore_wait(barrier, 2 * ((z + 1) * (y + 1) * (x + 1) - 1) + 1)
     for step in far_first:
         there, _, below = other(*step)
 
@@ -197,50 +217,81 @@
             signal(ready.at[chip], there * 2)
             signal(ready.at[chip], there * 2 + 1)
 
-    loads[0].wait()
-
-    def send_tokens(target):
+    with jax.named_scope("load_x"):
+        x_load.wait()
+
+    def remote(source, target, send, recv, device):
         pltpu.make_async_remote_copy(
-            src_ref=x_own.at[target],
-            dst_ref=gathered.at[me],
-            send_sem=send_a,
-            recv_sem=recv_a.at[z // 2],
-            device_id={"frame": target},
+            src_ref=source,
+            dst_ref=target,
+            send_sem=send,
+            recv_sem=recv,
+            device_id={"frame": device},
             device_id_type=MESH,
         ).start()
 
-    send_tokens(partner)
-    for step in far_first:
-        there, _, below = other(*step)
-
-        @pl.when(below)
+    group = me // half
+
+    def send_tokens(target):
+        remote(x_own.at[target], gathered.at[me], send_a, recv_a.at[group], target)
+
+    def send_extra(target):
+        remote(x_own.at[target + half], extra.at[me], send_x, recv_x, target)
+
+    with jax.named_scope("send_below"):
+        send_tokens(partner)
+        for step in far_first:
+            there, _, below = other(*step)
+
+            @pl.when(below)
+            def _():
+                send_tokens(there * 2)
+
+    with jax.named_scope("send_above"):
+        for step in near_first:
+            there, above, _ = other(*step)
+
+            @pl.when(above)
+            def _():
+                pl.semaphore_wait(ready.at[there], 2)
+                send_tokens(there * 2)
+
+    with jax.named_scope("send_rest"):
+        for step in near_first:
+            there, above, below = other(*step)
+
+            @pl.when(jnp.logical_not(above | below))
+            def _():
+                send_tokens(there * 2)
+
+        def send_late(level):
+            for there in reversed(range(chips)):
+                if there // 2 % 2 == level:
+
+                    @pl.when(there != chip)
+                    def _():
+                        send_tokens(there * 2 + 1)
+
+        def send_extras(to):
+            @pl.when(low)
+            def _():
+                for there in reversed(range(half // 2)):
+                    @pl.when(there * 2 + to != me)
+                    def _():
+                        send_extra(there * 2 + to)
+
+        send_late(0)
+        send_extras(1)
+        send_late(1)
+        send_extras(0)
+
+        @pl.when(low)
         def _():
-            send_tokens(there * 2)
-
-    for step in near_first:
-        there, above, _ = other(*step)
-
-        @pl.when(above)
-        def _():
-            pl.semaphore_wait(ready.at[there], 2)
-            send_tokens(there * 2)
-
-    for step in near_first:
-        there, above, below = other(*step)
-
-        @pl.when(jnp.logical_not(above | below))
-        def _():
-            send_tokens(there * 2)
-
-    for step in far_first:
-        there, _, _ = other(*step)
-        send_tokens(there * 2 + 1)
-    gathered[me] = x_own[me]
-    for load in loads[1:]:
-        load.wait()
-
-    half = devices // 2
-    rows = half * block
+            extra[me] = x_own[me + half]
+
+        gathered[me] = x_own[me]
+        for load in loads:
+            load.wait()
 
     def arrived(ref, semaphore):
         pltpu.make_async_remote_copy(
@@ -257,102 +308,187 @@
             src_ref=ref,
             dst_ref=ref,
             send_sem=semaphore,
-            recv_sem=recv_a.at[0],
+            recv_sem=recv_x,
             device_id={"frame": partner},
             device_id_type=MESH,
         ).wait_send()
 
-    def project(part):
-        tokens = gathered[pl.ds(part * half, half)].astype(jnp.float32).reshape(rows, width)
+    def project(tokens, places, ask=True):
+        tokens = tokens.astype(jnp.float32)
         normed = (quadratic_average_rescaling(tokens) * gain_ref[...].reshape(1, width)).astype(
             jnp.bfloat16
         )
-        q = jnp.dot(normed, wq[...], preferred_element_type=jnp.float32)
+        q = jnp.dot(normed, wq[...], preferred_element_type=jnp.float32) if ask else None
         k = jnp.dot(normed, wk[...], preferred_element_type=jnp.float32)
         v = jnp.dot(normed, wv[...], preferred_element_type=jnp.float32)
-        to = pl.ds(pl.multiple_of(part * rows, rows), rows)
         for h in range(HEADS_WIN):
             c = slice(h * CHANNELS_PER_ATT, (h + 1) * CHANNELS_PER_ATT)
-            q_rows[to, c] = (
-                quadratic_average_rescaling(q[:, c]) * sharp_ref[h] / math.sqrt(CHANNELS_PER_ATT)
-            ).astype(jnp.bfloat16)
-            k_rows[to, c] = quadratic_average_rescaling(k[:, c]).astype(jnp.bfloat16)
-            v_rows[to, c] = v[:, c].astype(jnp.bfloat16)
-
-    mine = z // 2
-    arrived(gathered.at[pl.ds(0, half - 1)], recv_a.at[mine])
-    project(mine)
-    arrived(gathered.at[pl.ds(0, half)], recv_a.at[1 - mine])
-    project(1 - mine)
-
-    total = devices * block
-
-    def ids(axis):
-        shape = (total, 1) if axis == 0 else (1, total)
-        r = lax.broadcasted_iota(jnp.int32, shape, axis)
+            ks = quadratic_average_rescaling(k[:, c]).astype(jnp.bfloat16)
+            vs = v[:, c].astype(jnp.bfloat16)
+            if ask:
+                qs = (
+                    quadratic_average_rescaling(q[:, c]) * sharp_ref[h] / math.sqrt(CHANNELS_PER_ATT)
+                ).astype(jnp.bfloat16)
+            for i, place in enumerate(places):
+                a = slice(i * rows, (i + 1) * rows)
+                b = slice(place * rows, (place + 1) * rows)
+                k_rows[b, c] = ks[a]
+                v_rows[b, c] = vs[a]
+                if ask:
+                    q_rows[b, c] = qs[a]
+
+    def ids(first, count, axis):
+        shape = (count, 1) if axis == 0 else (1, count)
+        r = first + lax.broadcasted_iota(jnp.int32, shape, axis)
         owner = r // block
         inner = r - owner * block
         return owner * local_frames + inner // positions, inner % positions
 
-    t_row, p_row = ids(0)
-    t_col, p_col = ids(1)
-    offset = t_row - t_col
-    inside = (p_row == p_col) & (offset >= 0) & (offset < WINDOW)
-    for h in range(HEADS_WIN):
-        c = slice(h * CHANNELS_PER_ATT, (h + 1) * CHANNELS_PER_ATT)
-        scores = lax.dot_general(
-            q_rows[:, c], k_rows[:, c], (((1,), (1,)), ((), ())), preferred_element_type=jnp.float32
-        )
-        weights = softmax_bf16(scores, inside)
-        attended = jnp.dot(weights, v_rows[:, c], preferred_element_type=jnp.float32)
-        outgoing[:, :, c] = attended.reshape(devices, block, CHANNELS_PER_ATT).astype(jnp.bfloat16)
+    def attend(asking, keys, target):
+        first, count = asking
+        start, length = keys
+        base = 2 * rows if start >= 2 * rows else 0
+        t_row, p_row = ids(first - base, count, 0)
+        t_col, p_col = ids(start - base, length, 1)
+        offset = t_row - t_col
+        inside = (p_row == p_col) & (offset >= 0) & (offset < WINDOW)
+        a, b = slice(first, first + count), slice(start, start + length)
+        heads = [slice(h * CHANNELS_PER_ATT, (h + 1) * CHANNELS_PER_ATT) for h in range(HEADS_WIN)]
+        scores = [
+            lax.dot_general(
+                q_rows[a, c],
+                k_rows[b, c],
+                (((1,), (1,)), ((), ())),
+                preferred_element_type=jnp.float32,
+            )
+            for c in heads
+        ]
+        weights = [softmax_bf16(s, inside) for s in scores]
+        attended = [
+            jnp.dot(w, v_rows[b, c], preferred_element_type=jnp.float32)
+            for w, c in zip(weights, heads)
+        ]
+        for c, part in zip(heads, attended):
+            target[:, :, c] = part.reshape(half, block, CHANNELS_PER_ATT).astype(jnp.bfloat16)
+
+    def tokens_of(part):
+        return gathered[part * half : (part + 1) * half].reshape(rows, width)
 
     def send_back(target):
-        pltpu.make_async_remote_copy(
-            src_ref=outgoing.at[target],
-            dst_ref=returned.at[side, chip],
-            send_sem=send_b,
-            recv_sem=recv_b.at[side],
-            device_id={"frame": target},
-            device_id_type=MESH,
-        ).start()
-
-    for step in far_first:
-        there, _, _ = other(*step)
-        send_back(there * 2)
-        send_back(there * 2 + 1)
-    send_back(partner)
-    returned[side, chip] = outgoing[me]
-
-    def finish(s):
-        mixed = returned[s].astype(jnp.float32).reshape(rows, HIGH).astype(jnp.bfloat16)
+        remote(outgoing.at[target], returned.at[me], send_b, recv_b.at[group], target)
+
+    def back_to_high():
+        for k in range(half // 2):
+            there = half // 2 + lax.rem(chip + k, half // 2)
+            for s in range(2):
+                target = there * 2 + s
+
+                @pl.when(target != me)
+                def _():
+                    send_back(target)
+
+    @pl.when(low)
+    def _():
+        with jax.named_scope("wait_own"):
+            arrived(gathered.at[pl.ds(0, half - 1)], recv_a.at[0])
+        with jax.named_scope("work_own"):
+            project(tokens_of(0), (0,))
+            attend((0, rows), (0, rows), outgoing.at[pl.ds(0, half)])
+            for k in range(1, half):
+                send_back(lax.rem(me + k, half))
+            returned[me] = outgoing[me]
+        def extras():
+            with jax.named_scope("wait_extra"):
+                arrived(extra.at[pl.ds(0, half - 1)], recv_x)
+            with jax.named_scope("work_extra"):
+                project(extra[...].reshape(rows, width), (2,))
+                attend((2 * rows, rows), (2 * rows, rows), outgoing_extra)
+                for k in range(1, half):
+                    target = lax.rem(me + k, half)
+                    remote(
+                        outgoing_extra.at[target],
+                        returned.at[me + half],
+                        send_c,
+                        recv_b.at[1],
+                        target,
+                    )
+                returned[me + half] = outgoing_extra[me]
+
+        pl.when(side == 1)(extras)
+        with jax.named_scope("wait_far"):
+            arrived(gathered.at[pl.ds(0, half)], recv_a.at[1])
+        with jax.named_scope("work_far"):
+            project(tokens_of(1), (1,))
+            attend((rows, rows), (0, 2 * rows), outgoing.at[pl.ds(half, half)])
+            back_to_high()
+        pl.when(side == 0)(extras)
+
+    @pl.when(jnp.logical_not(low))
+    def _():
+        with jax.named_scope("wait_own"):
+            arrived(gathered.at[pl.ds(0, half - 1)], recv_a.at[1])
+        with jax.named_scope("work_own"):
+            project(tokens_of(1), (1,))
+        with jax.named_scope("wait_far"):
+            arrived(gathered.at[pl.ds(0, half)], recv_a.at[0])
+        with jax.named_scope("work_far"):
+            project(tokens_of(0), (0,), ask=False)
+            attend((rows, rows), (0, 2 * rows), outgoing.at[pl.ds(half, half)])
+            back_to_high()
+            returned[me] = outgoing[me]
+
+    def finish(part):
+        span = slice(part * half, (part + 1) * half)
+        mixed = returned[span].reshape(rows, HIGH)
         summed = jnp.dot(mixed, wo[...], preferred_element_type=jnp.float32)
-        for k in range(chips):
-            j = 2 * k + s
+        for k in range(half):
+            j = part * half + k
             out_ref[j] = (
                 summed[k * block : (k + 1) * block] + x_own[j].astype(jnp.float32)
             ).astype(jnp.bfloat16)
 
-    for s in range(2):
-
-        @pl.when(side == s)
+    @pl.when(low)
+    def _():
+        with jax.named_scope("wait_b0"):
+            arrived(returned.at[pl.ds(0, half - 1)], recv_b.at[0])
+        with jax.named_scope("finish0"):
+            finish(0)
+        with jax.named_scope("wait_b1"):
+            arrived(returned.at[pl.ds(0, half - 1)], recv_b.at[1])
+        with jax.named_scope("finish1"):
+            finish(1)
+
+    @pl.when(jnp.logical_not(low))
+    def _():
+        with jax.named_scope("wait_b1"):
+            arrived(returned.at[pl.ds(0, half - 1)], recv_b.at[1])
+        with jax.named_scope("finish1"):
+            finish(1)
+        with jax.named_scope("wait_b0"):
+            arrived(returned.at[pl.ds(0, half)], recv_b.at[0])
+        with jax.named_scope("finish0"):
+            finish(0)
+
+    with jax.named_scope("departed"):
+        departed(x_own.at[pl.ds(0, devices - 1)], send_a)
+
+        @pl.when(low)
         def _():
-            arrived(returned.at[s, pl.ds(0, chips - 1)], recv_b.at[s])
-
-        @pl.when(side != s)
+            departed(x_own.at[pl.ds(0, half - 1)], send_x)
+            departed(outgoing.at[pl.ds(0, devices - 1)], send_b)
+            departed(outgoing_extra.at[pl.ds(0, half - 1)], send_c)
+
+        @pl.when(jnp.logical_not(low))
         def _():
-            arrived(returned.at[s], recv_b.at[s])
-
-        finish(s)
-    departed(x_own.at[pl.ds(0, devices - 1)], send_a)
-    departed(outgoing.at[pl.ds(0, devices - 1)], send_b)
+            departed(outgoing.at[pl.ds(0, half - 1)], send_b)
 
 
 def local_fused(devices, x, gain, wq, wk, wv, sharp, wo):
     local_frames, seq_len, width = x.shape
     positions = seq_len // devices
     block = local_frames * positions
-    total = devices * block
+    half = devices // 2
+    rows = half * block
     blocks = x.reshape(local_frames, devices, positions, width)
     blocks = blocks.transpose(1, 0, 2, 3).reshape(devices, block, width)
     vmem = pl.BlockSpec(memory_space=pltpu.VMEM)
@@ -361,24 +497,31 @@
     out = pl.pallas_call(
         functools.partial(fused, devices, local_frames),
         out_shape=pltpu.VMEM(blocks.shape, jnp.bfloat16),
-        in_specs=[pl.BlockSpec(memory_space=pltpu.SMEM), anywhere, vmem] + [anywhere] * 4,
+        in_specs=[anywhere] * 7,
         out_specs=vmem,
         scratch_shapes=[
+            pltpu.SMEM(sharp.shape, jnp.float32),
+            pltpu.VMEM(gain.shape, jnp.float32),
             pltpu.VMEM(blocks.shape, jnp.bfloat16),
             pltpu.VMEM(wq.shape, jnp.bfloat16),
             pltpu.VMEM(wk.shape, jnp.bfloat16),
             pltpu.VMEM(wv.shape, jnp.bfloat16),
             pltpu.VMEM(wo.shape, jnp.bfloat16),
             pltpu.VMEM(blocks.shape, jnp.bfloat16),
-            pltpu.VMEM((total, HIGH), jnp.bfloat16),
-            pltpu.VMEM((total, HIGH), jnp.bfloat16),
-            pltpu.VMEM((total, HIGH), jnp.bfloat16),
+            pltpu.VMEM((half, block, width), jnp.bfloat16),
+            pltpu.VMEM((3 * rows, HIGH), jnp.bfloat16),
+            pltpu.VMEM((3 * rows, HIGH), jnp.bfloat16),
+            pltpu.VMEM((3 * rows, HIGH), jnp.bfloat16),
             pltpu.VMEM((devices, block, HIGH), jnp.bfloat16),
-            pltpu.VMEM((2, devices // 2, block, HIGH), jnp.bfloat16),
-            dma((5,)),
+            pltpu.VMEM((half, block, HIGH), jnp.bfloat16),
+            pltpu.VMEM((devices, block, HIGH), jnp.bfloat16),
+            dma((7,)),
             pltpu.SemaphoreType.REGULAR((devices // 2,)),
             dma,
+            dma,
             dma((2,)),
+            dma,
+            dma,
             dma,
             dma((2,)),
         ],

time: 32.5 us -> 29.8 us (0.917)
  the two profiles are of different devices: /device:TPU:0 before, /device:TPU:25 now
where the time goes in v2:
time: 29.8 us; the launch traced here: 29.6 us
  Pallas kernels  28.8 us (97%)
  local copies, waits for them, and re-layouts  0.84 us (3%)
    pallas_call x1, Pallas kernels, local_fused(): pl.pallas_call(functools.partial(fused, devices, local_frames), out_shape...  28.8 us
    unnamed x1, local copies, waits for them, and re-layouts  0.84 us

profile of v2, /device:TPU:25, one launch (start us, length us, event | category | flops | bytes accessed | tf_op | source)
XLA Modules:
  0.0 29.6 jit_solution(13593607410466768665)
XLA Ops:
  0.0 28.8 %shard_map.73 = bf16[32,8,1280]{2,1,0:T(8,128)(2,1)S(1)} custom-call(f32[5]{0:T(128)} %sharp_hbm.1, bf16[32,8,1280]{2,1,0:T(8,128)(2,1)} %bitcast.3, f32[1280]{0:T(1024)} %gain_hbm.1, bf16[1280,640]{1,0:T(8,128)(2,1)} %wq_hbm.1, bf16[1280,640]{1,0:T(8,128)(2,1)} %wk_hbm.1, bf16[1280,640]{1,0:T(8,128)(2,1)} %wv_hbm.1, bf16[640,1280]{1,0:T(8,128)(2,1)} %wo_hbm.1), custom_call_target="tpu_custom_call" | custom-call | tf_op jit(solution)/shard_map/pallas_call | solution.py:497
  28.8 0.8 %copy.9 = bf16[1,256,1280]{2,1,0:T(8,128)(2,1)} copy(bf16[1,256,1280]{2,1,0:T(8,128)(2,1)S(1)} %bitcast.2) | data formatting | bytes 1310720

commit v3 on v2

--- a/solution.py
+++ b/solution.py
@@ -124,14 +124,15 @@
     wk_hbm,
     wv_hbm,
     wo_hbm,
-    out_ref,
+    done_ref,
+    left_ref,
+    x_own,
+    wo,
     sharp_ref,
     gain_ref,
-    x_own,
     wq,
     wk,
     wv,
-    wo,
     gathered,
     extra,
     q_rows,
@@ -236,60 +237,110 @@
         remote(x_own.at[target], gathered.at[me], send_a, recv_a.at[group], target)
 
     def send_extra(target):
-        remote(x_own.at[target + half], extra.at[me], send_x, recv_x, target)
-
-    with jax.named_scope("send_below"):
+        remote(x_own.at[target + 1 + half], extra.at[me], send_x, recv_x, target)
+
+    shelf = depth // 2
+    inner = z < shelf - 1
+
+    def send_four(there):
+        for s in range(2):
+            send_tokens(there * 2 + s)
+        send_extra(there * 2)
+
+    with jax.named_scope("send_first"):
         send_tokens(partner)
+
+        @pl.when(low & (side == 1))
+        def _():
+            send_extra(partner)
+
+        @pl.when(low & (side == 0))
+        def _():
+            extra[me] = x_own[me + 1 + half]
+
+        gathered[me] = x_own[me]
+
+    def plane(step):
+        return lax.rem(z + step[0], depth)
+
+    def each_below(act):
         for step in far_first:
             there, _, below = other(*step)
-
-            @pl.when(below)
-            def _():
-                send_tokens(there * 2)
-
-    with jax.named_scope("send_above"):
+            pl.when(below)(functools.partial(act, there))
+
+    def each_joined(wanted, act):
         for step in near_first:
+            dz, dy, dx = step
             there, above, _ = other(*step)
 
-            @pl.when(above)
+            @pl.when(above & wanted(step))
             def _():
                 pl.semaphore_wait(ready.at[there], 2)
-                send_tokens(there * 2)
-
-    with jax.named_scope("send_rest"):
-        for step in near_first:
-            there, above, below = other(*step)
-
-            @pl.when(jnp.logical_not(above | below))
-            def _():
-                send_tokens(there * 2)
-
-        def send_late(level):
-            for there in reversed(range(chips)):
-                if there // 2 % 2 == level:
-
-                    @pl.when(there != chip)
-                    def _():
-                        send_tokens(there * 2 + 1)
-
-        def send_extras(to):
+                act(there, step)
+                ty, tx = lax.rem(there // 2, 2), lax.rem(there, 2)
+                for p in range(depth) if dz == 0 else (None,):
+                    tz = there // 4 if p is None else p
+                    for ey in range(2 - dy):
+                        for ex in range(2 - dx):
+                            found = (y >= ey) & (x >= ex)
+                            if p is not None:
+                                found &= (p < z) | ((p == z) & (ey + ex > 0))
+                            elif ey + ex == 0:
+                                continue
+                            pl.when(found)(
+                                functools.partial(
+                                    act, tz * 4 + (ty - ey) * 2 + tx - ex, step
+                                )
+                            )
+
+    @pl.when(inner)
+    def _():
+        with jax.named_scope("send_group"):
+            each_below(send_four)
+            each_joined(lambda step: plane(step) < shelf, lambda there, step: send_four(there))
+
+        with jax.named_scope("send_across"):
+            each_joined(
+                lambda step: plane(step) >= shelf, lambda there, step: send_tokens(there * 2)
+            )
+            for step in near_first:
+                there, _, _ = other(*step)
+
+                @pl.when(plane(step) >= shelf)
+                def _():
+                    send_tokens(there * 2 + 1)
+
+    @pl.when(jnp.logical_not(inner))
+    def _():
+        with jax.named_scope("send_below"):
+            each_below(lambda there: send_tokens(there * 2))
+
+        with jax.named_scope("send_above"):
+            each_joined(lambda step: True, lambda there, step: send_tokens(there * 2))
+
+        with jax.named_scope("send_rest"):
+
             @pl.when(low)
             def _():
-                for there in reversed(range(half // 2)):
-                    @pl.when(there * 2 + to != me)
-                    def _():
-                        send_extra(there * 2 + to)
-
-        send_late(0)
-        send_extras(1)
-        send_late(1)
-        send_extras(0)
-
-        @pl.when(low)
-        def _():
-            extra[me] = x_own[me + half]
-
-        gathered[me] = x_own[me]
+                for k in range(1, half // 2):
+                    there = lax.rem(chip + k, half // 2)
+                    send_tokens(there * 2 + 1)
+                    send_extra(there * 2)
+
+            for i in range(depth):
+                tz = lax.rem((1 - group) * shelf + i, depth)
+                for dy in range(2):
+                    for dx in range(2):
+                        there, _, _ = other(lax.rem(tz - z + depth, depth), dy, dx)
+                        if i < shelf:
+                            send_tokens(there * 2 + 1)
+                        else:
+
+                            @pl.when(jnp.logical_not(low) & (there != chip))
+                            def _():
+                                send_tokens(there * 2 + 1)
+
+    with jax.named_scope("load_rest"):
         for load in loads:
             load.wait()
 
@@ -375,7 +426,7 @@
         return gathered[part * half : (part + 1) * half].reshape(rows, width)
 
     def send_back(target):
-        remote(outgoing.at[target], returned.at[me], send_b, recv_b.at[group], target)
+        remote(outgoing.at[target], returned.at[side, chip], send_b, recv_b.at[side], target)
 
     def back_to_high():
         for k in range(half // 2):
@@ -396,7 +447,7 @@
             attend((0, rows), (0, rows), outgoing.at[pl.ds(0, half)])
             for k in range(1, half):
                 send_back(lax.rem(me + k, half))
-            returned[me] = outgoing[me]
+            returned[side, chip] = outgoing[me]
         def extras():
             with jax.named_scope("wait_extra"):
                 arrived(extra.at[pl.ds(0, half - 1)], recv_x)
@@ -407,14 +458,13 @@
                     target = lax.rem(me + k, half)
                     remote(
                         outgoing_extra.at[target],
-                        returned.at[me + half],
+                        returned.at[1, chip + half // 2],
                         send_c,
                         recv_b.at[1],
                         target,
                     )
-                returned[me + half] = outgoing_extra[me]
-
-        pl.when(side == 1)(extras)
+                returned[1, chip + half // 2] = outgoing_extra[me]
+
         with jax.named_scope("wait_far"):
             arrived(gathered.at[pl.ds(0, half)], recv_a.at[1])
         with jax.named_scope("work_far"):
@@ -431,56 +481,96 @@
             project(tokens_of(1), (1,))
         with jax.named_scope("wait_far"):
             arrived(gathered.at[pl.ds(0, half)], recv_a.at[0])
-        with jax.named_scope("work_far"):
-            project(tokens_of(0), (0,), ask=False)
-            attend((rows, rows), (0, 2 * rows), outgoing.at[pl.ds(half, half)])
-            back_to_high()
-            returned[me] = outgoing[me]
-
-    def finish(part):
-        span = slice(part * half, (part + 1) * half)
-        mixed = returned[span].reshape(rows, HIGH)
-        summed = jnp.dot(mixed, wo[...], preferred_element_type=jnp.float32)
-        for k in range(half):
-            j = part * half + k
-            out_ref[j] = (
-                summed[k * block : (k + 1) * block] + x_own[j].astype(jnp.float32)
-            ).astype(jnp.bfloat16)
-
-    @pl.when(low)
-    def _():
-        with jax.named_scope("wait_b0"):
-            arrived(returned.at[pl.ds(0, half - 1)], recv_b.at[0])
-        with jax.named_scope("finish0"):
-            finish(0)
-        with jax.named_scope("wait_b1"):
-            arrived(returned.at[pl.ds(0, half - 1)], recv_b.at[1])
-        with jax.named_scope("finish1"):
-            finish(1)
-
-    @pl.when(jnp.logical_not(low))
-    def _():
-        with jax.named_scope("wait_b1"):
-            arrived(returned.at[pl.ds(0, half - 1)], recv_b.at[1])
-        with jax.named_scope("finish1"):
-            finish(1)
-        with jax.named_scope("wait_b0"):
-            arrived(returned.at[pl.ds(0, half)], recv_b.at[0])
-        with jax.named_scope("finish0"):
-            finish(0)
+
+        @pl.when(side == 0)
+        def _():
+            with jax.named_scope("work_far"):
+                project(tokens_of(0), (0,))
+                attend((0, rows), (0, rows), outgoing.at[pl.ds(0, half)])
+                for k in range(half):
+                    send_back(lax.rem(me + k, half))
+                attend((rows, rows), (0, 2 * rows), outgoing.at[pl.ds(half, half)])
+                back_to_high()
+
+        @pl.when(side == 1)
+        def _():
+            with jax.named_scope("work_far"):
+                project(tokens_of(0), (0,), ask=False)
+                attend((rows, rows), (0, 2 * rows), outgoing.at[pl.ds(half, half)])
+                back_to_high()
+
+        returned[side, chip] = outgoing[me]
+
+    for s in range(2):
+        with jax.named_scope(f"wait_b{s}"):
+            fewer = (side == s) | low if s else side == s
+
+            @pl.when(fewer)
+            def _():
+                arrived(returned.at[s, pl.ds(0, half - 1)], recv_b.at[s])
+
+            @pl.when(jnp.logical_not(fewer))
+            def _():
+                arrived(returned.at[s], recv_b.at[s])
+
+        with jax.named_scope(f"finish{s}"):
+            if s:
+                left_ref[...] = returned[s].reshape(rows, HIGH)
+            else:
+                summed = jnp.dot(
+                    returned[s].reshape(rows, HIGH), wo[...], preferred_element_type=jnp.float32
+                )
+                for k in range(half):
+                    done_ref[k] = (
+                        summed[k * block : (k + 1) * block] + x_own[2 * k].astype(jnp.float32)
+                    ).astype(jnp.bfloat16)
 
     with jax.named_scope("departed"):
         departed(x_own.at[pl.ds(0, devices - 1)], send_a)
 
-        @pl.when(low)
-        def _():
-            departed(x_own.at[pl.ds(0, half - 1)], send_x)
+        @pl.when(low & (side == 0))
+        def _():
+            departed(x_own.at[pl.ds(0, half // 2 - 1)], send_x)
+            departed(outgoing_extra.at[pl.ds(0, half - 1)], send_c)
+
+        @pl.when(low & (side == 1))
+        def _():
+            departed(x_own.at[pl.ds(0, half // 2)], send_x)
+
+        @pl.when(low | (side == 0))
+        def _():
             departed(outgoing.at[pl.ds(0, devices - 1)], send_b)
-            departed(outgoing_extra.at[pl.ds(0, half - 1)], send_c)
-
-        @pl.when(jnp.logical_not(low))
+
+        @pl.when(jnp.logical_not(low) & (side == 1))
         def _():
             departed(outgoing.at[pl.ds(0, half - 1)], send_b)
+
+
+def finish(done, left, x_own, wo, result, held, sem):
+    half, block, width = done.shape
+    first = pltpu.make_async_copy(done, result.at[:, 0], sem.at[0])
+    first.start()
+    pieces = sem.shape[0] - 1
+    share = width // pieces
+    copies = []
+    for n in range(pieces):
+        c = slice(n * share, (n + 1) * share)
+        summed = jnp.dot(left[...], wo[:, c], preferred_element_type=jnp.float32)
+        for k in range(half):
+            held[k, :, c] = (
+                summed[k * block : (k + 1) * block] + x_own[2 * k + 1, :, c].astype(jnp.float32)
+            ).astype(jnp.bfloat16)
+        copies.append(
+            pltpu.make_async_copy(
+                held.at[:, :, pl.ds(n * share, share)],
+                result.at[:, 1, :, pl.ds(n * share, share)],
+                sem.at[n + 1],
+            )
+        )
+        copies[-1].start()
+    first.wait()
+    for copy in copies:
+        copy.wait()
 
 
 def local_fused(devices, x, gain, wq, wk, wv, sharp, wo):
@@ -494,19 +584,23 @@
     vmem = pl.BlockSpec(memory_space=pltpu.VMEM)
     anywhere = pl.BlockSpec(memory_space=pl.ANY)
     dma = pltpu.SemaphoreType.DMA
-    out = pl.pallas_call(
+    held = (half, block, width)
+    parts = pl.pallas_call(
         functools.partial(fused, devices, local_frames),
-        out_shape=pltpu.VMEM(blocks.shape, jnp.bfloat16),
+        out_shape=[
+            pltpu.VMEM(held, jnp.bfloat16),
+            pltpu.VMEM((rows, HIGH), jnp.bfloat16),
+            pltpu.VMEM(blocks.shape, jnp.bfloat16),
+            pltpu.VMEM(wo.shape, jnp.bfloat16),
+        ],
         in_specs=[anywhere] * 7,
-        out_specs=vmem,
+        out_specs=[vmem] * 4,
         scratch_shapes=[
             pltpu.SMEM(sharp.shape, jnp.float32),
             pltpu.VMEM(gain.shape, jnp.float32),
-            pltpu.VMEM(blocks.shape, jnp.bfloat16),
             pltpu.VMEM(wq.shape, jnp.bfloat16),
             pltpu.VMEM(wk.shape, jnp.bfloat16),
             pltpu.VMEM(wv.shape, jnp.bfloat16),
-            pltpu.VMEM(wo.shape, jnp.bfloat16),
             pltpu.VMEM(blocks.shape, jnp.bfloat16),
             pltpu.VMEM((half, block, width), jnp.bfloat16),
             pltpu.VMEM((3 * rows, HIGH), jnp.bfloat16),
@@ -514,7 +608,7 @@
             pltpu.VMEM((3 * rows, HIGH), jnp.bfloat16),
             pltpu.VMEM((devices, block, HIGH), jnp.bfloat16),
             pltpu.VMEM((half, block, HIGH), jnp.bfloat16),
-            pltpu.VMEM((devices, block, HIGH), jnp.bfloat16),
+            pltpu.VMEM((2, half, block, HIGH), jnp.bfloat16),
             dma((7,)),
             pltpu.SemaphoreType.REGULAR((devices // 2,)),
             dma,
@@ -529,6 +623,13 @@
             collective_id=0, has_side_effects=True, vmem_limit_bytes=60 * 2**20
         ),
     )(sharp, blocks, gain, wq, wk, wv, wo)
+    out = pl.pallas_call(
+        finish,
+        out_shape=jax.ShapeDtypeStruct((half, 2, block, width), jnp.bfloat16),
+        in_specs=[vmem] * 4,
+        out_specs=anywhere,
+        scratch_shapes=[pltpu.VMEM(held, jnp.bfloat16), dma((3,))],
+    )(*[pltpu.with_memory_space_constraint(part, pltpu.VMEM) for part in parts])
     out = out.reshape(devices, local_frames, positions, width).transpose(1, 0, 2, 3)
     return out.reshape(x.shape)
 

time: 29.8 us -> 28.2 us (0.946)
  local copies, waits for them, and re-layouts: 0.84 us -> 0 us
  Pallas kernels: 28.8 us -> 28.1 us
    pallas_call x1, Pallas kernels: 28.8 us -> 26.9 us  [local_fused(): pl.pallas_call(functools.partial(fused, devices, local_frames), out_shape...]
    pallas_call x0 -> x1, Pallas kernels: none -> 1.17 us  [local_fused(): pl.pallas_call(finish, out_shape=jax.ShapeDtypeStruct((half, 2, block, wi...]
    unnamed x1 -> x0, local copies, waits for them, and re-layouts: 0.84 us -> none
where the time goes in v3:
time: 28.2 us; the launch traced here: 28.1 us
  Pallas kernels  28.1 us (100%)
    pallas_call x1, Pallas kernels, local_fused(): pl.pallas_call(functools.partial(fused, devices, local_frames), out_shape...  26.9 us
    pallas_call x1, Pallas kernels, local_fused(): pl.pallas_call(finish, out_shape=jax.ShapeDtypeStruct((half, 2, block, wi...  1.17 us

profile of v3, /device:TPU:25, one launch (start us, length us, event | category | flops | bytes accessed | tf_op | source)
XLA Modules:
  0.0 28.1 jit_solution(2131463876097472426)
XLA Ops:
  0.0 26.9 %shard_map.73 = (bf16[16,8,1280]{2,1,0:T(8,128)(2,1)S(1)}, bf16[128,640]{1,0:T(8,128)(2,1)S(1)}, bf16[32,8,1280]{2,1,0:T(8,128)(2,1)S(1)}, bf16[640,1280]{1,0:T(8,128)(2,1)S(1)}) custom-call(f32[5]{0:T(128)} %sharp_hbm.1, bf16[32,8,1280]{2,1,0:T(8,128)(2,1)} %bitcast.2, f32[1280]{0:T(1024)} %gain_hbm.1, bf16[1280,640]{1,0:T(8,128)(2,1)} %wq_hbm.1, ...), custom_call_target="tpu_custom_call" | custom-call | tf_op jit(solution)/shard_map/pallas_call | solution.py:588
  26.9 1.2 %shard_map.74 = bf16[16,2,8,1280]{3,2,1,0:T(8,128)(2,1)} custom-call(bf16[16,8,1280]{2,1,0:T(8,128)(2,1)S(1)} %get-tuple-element.9.done, bf16[128,640]{1,0:T(8,128)(2,1)S(1)} %get-tuple-element.10.left, bf16[32,8,1280]{2,1,0:T(8,128)(2,1)S(1)} %get-tuple-element.11.x_own, bf16[640,1280]{1,0:T(8,128)(2,1)S(1)} %get-tuple-element.12.wo), custom_call_target="tpu_custom_call" | custom-call | tf_op jit(solution)/shard_map/pallas_call | solution.py:626

commit v4 on v3

--- a/solution.py
+++ b/solution.py
@@ -231,10 +231,11 @@
             device_id_type=MESH,
         ).start()
 
-    group = me // half
+    layer = devices // depth
+    layer_rows = layer * block
 
     def send_tokens(target):
-        remote(x_own.at[target], gathered.at[me], send_a, recv_a.at[group], target)
+        remote(x_own.at[target], gathered.at[me], send_a, recv_a.at[z], target)
 
     def send_extra(target):
         remote(x_own.at[target + 1 + half], extra.at[me], send_x, recv_x, target)
@@ -328,17 +329,15 @@
                     send_extra(there * 2)
 
             for i in range(depth):
-                tz = lax.rem((1 - group) * shelf + i, depth)
+                upward = jnp.where(z == depth - 1, (i + shelf) % depth, i)
+                tz = jnp.where(low, (i + shelf) % depth, upward)
                 for dy in range(2):
                     for dx in range(2):
                         there, _, _ = other(lax.rem(tz - z + depth, depth), dy, dx)
-                        if i < shelf:
+
+                        @pl.when((there != chip) & (jnp.logical_not(low) | (tz >= shelf)))
+                        def _():
                             send_tokens(there * 2 + 1)
-                        else:
-
-                            @pl.when(jnp.logical_not(low) & (there != chip))
-                            def _():
-                                send_tokens(there * 2 + 1)
 
     with jax.named_scope("load_rest"):
         for load in loads:
@@ -364,29 +363,23 @@
             device_id_type=MESH,
         ).wait_send()
 
-    def project(tokens, places, ask=True):
-        tokens = tokens.astype(jnp.float32)
+    def project(tokens, place, ask=True):
+        tokens = tokens.reshape(-1, width).astype(jnp.float32)
         normed = (quadratic_average_rescaling(tokens) * gain_ref[...].reshape(1, width)).astype(
             jnp.bfloat16
         )
         q = jnp.dot(normed, wq[...], preferred_element_type=jnp.float32) if ask else None
         k = jnp.dot(normed, wk[...], preferred_element_type=jnp.float32)
         v = jnp.dot(normed, wv[...], preferred_element_type=jnp.float32)
+        b = slice(place, place + tokens.shape[0])
         for h in range(HEADS_WIN):
             c = slice(h * CHANNELS_PER_ATT, (h + 1) * CHANNELS_PER_ATT)
-            ks = quadratic_average_rescaling(k[:, c]).astype(jnp.bfloat16)
-            vs = v[:, c].astype(jnp.bfloat16)
             if ask:
-                qs = (
+                q_rows[b, c] = (
                     quadratic_average_rescaling(q[:, c]) * sharp_ref[h] / math.sqrt(CHANNELS_PER_ATT)
                 ).astype(jnp.bfloat16)
-            for i, place in enumerate(places):
-                a = slice(i * rows, (i + 1) * rows)
-                b = slice(place * rows, (place + 1) * rows)
-                k_rows[b, c] = ks[a]
-                v_rows[b, c] = vs[a]
-                if ask:
-                    q_rows[b, c] = qs[a]
+            k_rows[b, c] = quadratic_average_rescaling(k[:, c]).astype(jnp.bfloat16)
+            v_rows[b, c] = v[:, c].astype(jnp.bfloat16)
 
     def ids(first, count, axis):
         shape = (count, 1) if axis == 0 else (1, count)
@@ -420,17 +413,16 @@
             for w, c in zip(weights, heads)
         ]
         for c, part in zip(heads, attended):
-            target[:, :, c] = part.reshape(half, block, CHANNELS_PER_ATT).astype(jnp.bfloat16)
-
-    def tokens_of(part):
-        return gathered[part * half : (part + 1) * half].reshape(rows, width)
+            target[:, :, c] = part.reshape(count // block, block, CHANNELS_PER_ATT).astype(
+                jnp.bfloat16
+            )
 
     def send_back(target):
         remote(outgoing.at[target], returned.at[side, chip], send_b, recv_b.at[side], target)
 
-    def back_to_high():
-        for k in range(half // 2):
-            there = half // 2 + lax.rem(chip + k, half // 2)
+    def back_to_layer(p):
+        for k in range(layer // 2):
+            there = p * (layer // 2) + lax.rem(chip + k, layer // 2)
             for s in range(2):
                 target = there * 2 + s
 
@@ -438,21 +430,47 @@
                 def _():
                     send_back(target)
 
+    def wait_layer(p):
+        @pl.when(z == p)
+        def _():
+            arrived(gathered.at[pl.ds(0, layer - 1)], recv_a.at[p])
+
+        @pl.when(z != p)
+        def _():
+            arrived(gathered.at[pl.ds(0, layer)], recv_a.at[p])
+
+    lower, upper = range(shelf), range(shelf, depth)
+
     @pl.when(low)
     def _():
         with jax.named_scope("wait_own"):
-            arrived(gathered.at[pl.ds(0, half - 1)], recv_a.at[0])
+            for p in lower:
+                wait_layer(p)
         with jax.named_scope("work_own"):
-            project(tokens_of(0), (0,))
+            project(gathered[:half], 0)
             attend((0, rows), (0, rows), outgoing.at[pl.ds(0, half)])
             for k in range(1, half):
                 send_back(lax.rem(me + k, half))
             returned[side, chip] = outgoing[me]
-        def extras():
+
+        for p in upper:
+            with jax.named_scope(f"wait_far{p}"):
+                wait_layer(p)
+            with jax.named_scope(f"work_far{p}"):
+                project(gathered[p * layer : (p + 1) * layer], p * layer_rows)
+                attend(
+                    (p * layer_rows, layer_rows),
+                    (0, (p + 1) * layer_rows),
+                    outgoing.at[pl.ds(p * layer, layer)],
+                )
+                back_to_layer(p)
+
+        @pl.when(side == 0)
+        def _():
             with jax.named_scope("wait_extra"):
                 arrived(extra.at[pl.ds(0, half - 1)], recv_x)
             with jax.named_scope("work_extra"):
-                project(extra[...].reshape(rows, width), (2,))
+                project(extra[...], 2 * rows)
                 attend((2 * rows, rows), (2 * rows, rows), outgoing_extra)
                 for k in range(1, half):
                     target = lax.rem(me + k, half)
@@ -465,39 +483,35 @@
                     )
                 returned[1, chip + half // 2] = outgoing_extra[me]
 
-        with jax.named_scope("wait_far"):
-            arrived(gathered.at[pl.ds(0, half)], recv_a.at[1])
-        with jax.named_scope("work_far"):
-            project(tokens_of(1), (1,))
-            attend((rows, rows), (0, 2 * rows), outgoing.at[pl.ds(half, half)])
-            back_to_high()
-        pl.when(side == 0)(extras)
-
     @pl.when(jnp.logical_not(low))
     def _():
         with jax.named_scope("wait_own"):
-            arrived(gathered.at[pl.ds(0, half - 1)], recv_a.at[1])
+            for p in upper:
+                wait_layer(p)
         with jax.named_scope("work_own"):
-            project(tokens_of(1), (1,))
+            project(gathered[half:], rows)
         with jax.named_scope("wait_far"):
-            arrived(gathered.at[pl.ds(0, half)], recv_a.at[0])
+            for p in lower:
+                wait_layer(p)
 
         @pl.when(side == 0)
         def _():
             with jax.named_scope("work_far"):
-                project(tokens_of(0), (0,))
+                project(gathered[:half], 0)
                 attend((0, rows), (0, rows), outgoing.at[pl.ds(0, half)])
                 for k in range(half):
                     send_back(lax.rem(me + k, half))
                 attend((rows, rows), (0, 2 * rows), outgoing.at[pl.ds(half, half)])
-                back_to_high()
+                for p in upper:
+                    back_to_layer(p)
 
         @pl.when(side == 1)
         def _():
             with jax.named_scope("work_far"):
-                project(tokens_of(0), (0,), ask=False)
+                project(gathered[:half], 0, ask=False)
                 attend((rows, rows), (0, 2 * rows), outgoing.at[pl.ds(half, half)])
-                back_to_high()
+                for p in upper:
+                    back_to_layer(p)
 
         returned[side, chip] = outgoing[me]
 
@@ -613,7 +627,7 @@
             pltpu.SemaphoreType.REGULAR((devices // 2,)),
             dma,
             dma,
-            dma((2,)),
+            dma((devices // 8,)),
             dma,
             dma,
             dma,

time: 28.2 us -> 27.7 us (0.982)
  Pallas kernels: 28.1 us -> 27.6 us
    pallas_call x1, Pallas kernels: 26.9 us -> 26.4 us  [local_fused(): pl.pallas_call(functools.partial(fused, devices, local_frames), out_shape...]
where the time goes in v4:
time: 27.7 us; the launch traced here: 27.6 us
  Pallas kernels  27.6 us (100%)
    pallas_call x1, Pallas kernels, local_fused(): pl.pallas_call(functools.partial(fused, devices, local_frames), out_shape...  26.4 us
    pallas_call x1, Pallas kernels, local_fused(): pl.pallas_call(finish, out_shape=jax.ShapeDtypeStruct((half, 2, block, wi...  1.17 us

profile of v4, /device:TPU:25, one launch (start us, length us, event | category | flops | bytes accessed | tf_op | source)
XLA Modules:
  0.0 27.6 jit_solution(144095004289919279)
XLA Ops:
  0.0 26.4 %shard_map.73 = (bf16[16,8,1280]{2,1,0:T(8,128)(2,1)S(1)}, bf16[128,640]{1,0:T(8,128)(2,1)S(1)}, bf16[32,8,1280]{2,1,0:T(8,128)(2,1)S(1)}, bf16[640,1280]{1,0:T(8,128)(2,1)S(1)}) custom-call(f32[5]{0:T(128)} %sharp_hbm.1, bf16[32,8,1280]{2,1,0:T(8,128)(2,1)} %bitcast.2, f32[1280]{0:T(1024)} %gain_hbm.1, bf16[1280,640]{1,0:T(8,128)(2,1)} %wq_hbm.1, ...), custom_call_target="tpu_custom_call" | custom-call | tf_op jit(solution)/shard_map/pallas_call | solution.py:602
  26.4 1.2 %shard_map.74 = bf16[16,2,8,1280]{3,2,1,0:T(8,128)(2,1)} custom-call(bf16[16,8,1280]{2,1,0:T(8,128)(2,1)S(1)} %get-tuple-element.9.done, bf16[128,640]{1,0:T(8,128)(2,1)S(1)} %get-tuple-element.10.left, bf16[32,8,1280]{2,1,0:T(8,128)(2,1)S(1)} %get-tuple-element.11.x_own, bf16[640,1280]{1,0:T(8,128)(2,1)S(1)} %get-tuple-element.12.wo), custom_call_target="tpu_custom_call" | custom-call | tf_op jit(solution)/shard_map/pallas_call | solution.py:640

commit v5 on v4

--- a/solution.py
+++ b/solution.py
@@ -453,17 +453,18 @@
                 send_back(lax.rem(me + k, half))
             returned[side, chip] = outgoing[me]
 
-        for p in upper:
+        for p in reversed(upper):
             with jax.named_scope(f"wait_far{p}"):
                 wait_layer(p)
             with jax.named_scope(f"work_far{p}"):
                 project(gathered[p * layer : (p + 1) * layer], p * layer_rows)
-                attend(
-                    (p * layer_rows, layer_rows),
-                    (0, (p + 1) * layer_rows),
-                    outgoing.at[pl.ds(p * layer, layer)],
-                )
-                back_to_layer(p)
+        with jax.named_scope("work_back"):
+            attend((rows, rows), (0, 2 * rows), outgoing.at[pl.ds(half, half)])
+            for k in range(layer // 2):
+                for p in upper:
+                    there = p * (layer // 2) + lax.rem(chip + k, layer // 2)
+                    send_back(there * 2)
+                    send_back(there * 2 + 1)
 
         @pl.when(side == 0)
         def _():

time: 27.7 us -> 27.5 us (level)
  Pallas kernels: 27.6 us -> 27.3 us
    pallas_call x1, Pallas kernels: 26.4 us -> 26.1 us  [local_fused(): pl.pallas_call(functools.partial(fused, devices, local_frames), out_shape...]
where the time goes in v5:
time: 27.5 us; the launch traced here: 27.3 us
  Pallas kernels  27.3 us (99%)
    pallas_call x1, Pallas kernels, local_fused(): pl.pallas_call(functools.partial(fused, devices, local_frames), out_shape...  26.1 us
    pallas_call x1, Pallas kernels, local_fused(): pl.pallas_call(finish, out_shape=jax.ShapeDtypeStruct((half, 2, block, wi...  1.17 us

profile of v5, /device:TPU:25, one launch (start us, length us, event | category | flops | bytes accessed | tf_op | source)
XLA Modules:
  0.0 27.3 jit_solution(2451105802410787533)
XLA Ops:
  0.0 26.1 %shard_map.73 = (bf16[16,8,1280]{2,1,0:T(8,128)(2,1)S(1)}, bf16[128,640]{1,0:T(8,128)(2,1)S(1)}, bf16[32,8,1280]{2,1,0:T(8,128)(2,1)S(1)}, bf16[640,1280]{1,0:T(8,128)(2,1)S(1)}) custom-call(f32[5]{0:T(128)} %sharp_hbm.1, bf16[32,8,1280]{2,1,0:T(8,128)(2,1)} %bitcast.2, f32[1280]{0:T(1024)} %gain_hbm.1, bf16[1280,640]{1,0:T(8,128)(2,1)} %wq_hbm.1, ...), custom_call_target="tpu_custom_call" | custom-call | tf_op jit(solution)/shard_map/pallas_call | solution.py:603
  26.1 1.2 %shard_map.74 = bf16[16,2,8,1280]{3,2,1,0:T(8,128)(2,1)} custom-call(bf16[16,8,1280]{2,1,0:T(8,128)(2,1)S(1)} %get-tuple-element.9.done, bf16[128,640]{1,0:T(8,128)(2,1)S(1)} %get-tuple-element.10.left, bf16[32,8,1280]{2,1,0:T(8,128)(2,1)S(1)} %get-tuple-element.11.x_own, bf16[640,1280]{1,0:T(8,128)(2,1)S(1)} %get-tuple-element.12.wo), custom_call_target="tpu_custom_call" | custom-call | tf_op jit(solution)/shard_map/pallas_call | solution.py:641

commit v6 on v5

--- a/solution.py
+++ b/solution.py
@@ -52,7 +52,7 @@
     scores = jnp.where(window_mask, scores, -1e30)
     top = jnp.max(scores, axis=-1, keepdims=True)
     expo = jnp.exp(scores - top)
-    return (expo / jnp.sum(expo, axis=-1, keepdims=True)).astype(jnp.bfloat16)
+    return (expo * (1.0 / jnp.sum(expo, axis=-1, keepdims=True))).astype(jnp.bfloat16)
 
 
 def band_attention(asking_token_vectors, key_matrix_rows, value_matrix_rows):

time: 27.5 us -> 27.5 us (level)
  no operation moved by 1% of the time
where the time goes in v6:
time: 27.5 us; the launch traced here: 27.3 us
  Pallas kernels  27.3 us (99%)
    pallas_call x1, Pallas kernels, local_fused(): pl.pallas_call(functools.partial(fused, devices, local_frames), out_shape...  26.1 us
    pallas_call x1, Pallas kernels, local_fused(): pl.pallas_call(finish, out_shape=jax.ShapeDtypeStruct((half, 2, block, wi...  1.17 us

profile of v6, /device:TPU:25, one launch (start us, length us, event | category | flops | bytes accessed | tf_op | source)
XLA Modules:
  0.0 27.3 jit_solution(2451105802410787533)
XLA Ops:
  0.0 26.1 %shard_map.73 = (bf16[16,8,1280]{2,1,0:T(8,128)(2,1)S(1)}, bf16[128,640]{1,0:T(8,128)(2,1)S(1)}, bf16[32,8,1280]{2,1,0:T(8,128)(2,1)S(1)}, bf16[640,1280]{1,0:T(8,128)(2,1)S(1)}) custom-call(f32[5]{0:T(128)} %sharp_hbm.1, bf16[32,8,1280]{2,1,0:T(8,128)(2,1)} %bitcast.2, f32[1280]{0:T(1024)} %gain_hbm.1, bf16[1280,640]{1,0:T(8,128)(2,1)} %wq_hbm.1, ...), custom_call_target="tpu_custom_call" | custom-call | tf_op jit(solution)/shard_map/pallas_call | solution.py:603
  26.1 1.2 %shard_map.74 = bf16[16,2,8,1280]{3,2,1,0:T(8,128)(2,1)} custom-call(bf16[16,8,1280]{2,1,0:T(8,128)(2,1)S(1)} %get-tuple-element.9.done, bf16[128,640]{1,0:T(8,128)(2,1)S(1)} %get-tuple-element.10.left, bf16[32,8,1280]{2,1,0:T(8,128)(2,1)S(1)} %get-tuple-element.11.x_own, bf16[640,1280]{1,0:T(8,128)(2,1)S(1)} %get-tuple-element.12.wo), custom_call_target="tpu_custom_call" | custom-call | tf_op jit(solution)/shard_map/pallas_call | solution.py:641
